TPU v7x, 8 devices: a whole 2x2x1 slice. The times are simulated.
8 devices in a mesh: dp: 2 (over z, y), tp: 4 (over x, core).
Axes of the slice: x: 2, y: 2, z: 1, core: 2. Of those that a mesh axis runs over, the one named last changes fastest.
Arguments:
- x_in: bfloat16 [256, 6656], P('dp', 'tp'), parts along dimension 0
- w_cross: bfloat16 [3, 6656, 6656], P(None, None, 'tp')
- b_cross: float32 [3, 6656], P(None, 'tp')
Outputs:
- output: bfloat16 [256, 6656], P('dp', 'tp'), parts along dimension 0
There are 2 independent parts. A program takes and returns all parts, laid end to end along the dimension named above; an argument that names none is the same for every part.
All inputs are finite; a program needn't handle non-finite values.
Results may differ from a plain program's by a relative error of at most 0.00176.
Values are sent between devices in bfloat16 or wider.
A program may use at most 1 GiB of HBM per device.

v0:
```python
import jax
import jax.numpy as jnp
from jax import lax
from jax.sharding import PartitionSpec as P


def solution(mesh):
    def local_stack(x_loc, w_loc, b_loc):
        x_first = x_loc.astype(jnp.float32)
        x_cur = x_loc
        for layer_idx in range(w_loc.shape[0]):
            x_full = lax.all_gather(x_cur, "tp", axis=1, tiled=True)
            projected = jnp.dot(x_full, w_loc[layer_idx], preferred_element_type=jnp.float32)
            x_cur = (x_first * (projected + b_loc[layer_idx]) + x_cur.astype(jnp.float32)).astype(jnp.bfloat16)
        return x_cur

    return jax.shard_map(
        local_stack,
        mesh=mesh,
        in_specs=(P("dp", "tp"), P(None, None, "tp"), P(None, "tp")),
        out_specs=P("dp", "tp"),
        check_vma=False,
    )
```

profile of v0, /device:TPU:1, one launch (start us, length us, event | category | flops | bytes accessed | tf_op | source)
XLA Modules:
  0.0 105.8 jit_solution(8881104837768202645)
XLA Ops:
  6.5 0.0 all-gather.4.cloned.1.call-start
  6.5 0.7 all-gather.4.cloned.1.call-update
  7.3 0.0 all-gather.6.cloned.1.call-start
  7.3 0.9 slice_reduce_fusion
  8.2 20.2 %all-gather.4.cloned.1.call-done = bf16[128,6656]{1,0:T(8,128)(2,1)} async-done(((bf16[128,1664]{1,0:T(8,128)(2,1)}), bf16[128,6656]{1,0:T(8,128)(2,1)}) %all-gather.4.cloned.1.call-update) | async-done | bytes 1703952 | tf_op jit(solution)/shard_map/all_gather | solution.py:12
  28.4 0.0 copy-start
  28.4 11.9 %fusion.36 = bf16[128,1664]{1,0:T(8,128)(2,1)} fusion(bf16[128,6656]{1,0:T(8,128)(2,1)} %all-gather.4.cloned.1.call-done, bf16[3,6656,1664]{2,1,0:T(8,128)(2,1)} %param.4, bf16[128,1664]{1,0:T(8,128)(2,1)} %param.3, f32[1664]{0:T(1024)S(1)} %get-tuple-element.6), kind=kOutput, calls=%fused_computation.18 | convolution fusion | flops 2836414464 | bytes 24713728 | tf_op jit(solution)/shard_map/dot_general | solution.py:13
  40.3 0.0 all-gather.6.cloned.1.call-update
  40.3 0.0 all-gather.8.cloned.1.call-start
  40.4 17.5 %all-gather.6.cloned.1.call-done = bf16[128,6656]{1,0:T(8,128)(2,1)} async-done(((bf16[128,1664]{1,0:T(8,128)(2,1)}), bf16[128,6656]{1,0:T(8,128)(2,1)}) %all-gather.6.cloned.1.call-update) | async-done | bytes 1703952 | tf_op jit(solution)/shard_map/all_gather | solution.py:12
  57.9 0.0 copy-done
  57.9 11.9 %fusion.39 = bf16[128,1664]{1,0:T(8,128)(2,1)} fusion(bf16[128,6656]{1,0:T(8,128)(2,1)} %all-gather.6.cloned.1.call-done, bf16[3,6656,1664]{2,1,0:T(8,128)(2,1)} %param.4, bf16[128,1664]{1,0:T(8,128)(2,1)S(1)} %copy-done, bf16[128,1664]{1,0:T(8,128)(2,1)} %fusion.36, f32[1664]{0:T(1024)S(1)} %get-tuple-element.7), kind=kOutput, calls=%fused_computation.19 | convolution fusion | flops 2836627456 | bytes 25139712 | tf_op jit(solution)/shard_map/dot_general | solution.py:13
  69.8 0.0 all-gather.8.cloned.1.call-update
  69.8 17.5 %all-gather.8.cloned.1.call-done = bf16[128,6656]{1,0:T(8,128)(2,1)} async-done(((bf16[128,1664]{1,0:T(8,128)(2,1)}), bf16[128,6656]{1,0:T(8,128)(2,1)}) %all-gather.8.cloned.1.call-update) | async-done | bytes 1703952 | tf_op jit(solution)/shard_map/all_gather | solution.py:12
  87.3 11.9 %fusion.42 = bf16[128,1664]{1,0:T(8,128)(2,1)} fusion(bf16[128,6656]{1,0:T(8,128)(2,1)} %all-gather.8.cloned.1.call-done, bf16[3,6656,1664]{2,1,0:T(8,128)(2,1)} %param.4, bf16[128,1664]{1,0:T(8,128)(2,1)S(1)} %copy-done, bf16[128,1664]{1,0:T(8,128)(2,1)} %fusion.39, f32[1664]{0:T(1024)S(1)} %get-tuple-element.5), kind=kOutput, calls=%fused_computation.20 | convolution fusion | flops 2836627456 | bytes 25139712 | tf_op jit(solution)/shard_map/dot_general | solution.py:13
Async XLA Ops:
  6.5 21.9 %all-gather.4.cloned.1.call-start = ((), (), s32[]{:S(2)}) async-start(), calls=%async_computation | async-start | bytes 2129920 | tf_op jit(solution)/shard_map/all_gather | solution.py:12
  7.3 50.6 %all-gather.6.cloned.1.call-start = ((), (), s32[]{:S(2)}) async-start(), calls=%async_computation.1 | async-start | bytes 2129920 | tf_op jit(solution)/shard_map/all_gather | solution.py:12
  28.4 29.4 %copy-start = (bf16[128,1664]{1,0:T(8,128)(2,1)S(1)}, bf16[128,1664]{1,0:T(8,128)(2,1)}, u32[]{:S(2)}) copy-start(bf16[128,1664]{1,0:T(8,128)(2,1)} %param.3) | copy-start | bytes 1277956
  40.3 47.0 %all-gather.8.cloned.1.call-start = ((), (), s32[]{:S(2)}) async-start(), calls=%async_computation.2 | async-start | bytes 2129920 | tf_op jit(solution)/shard_map/all_gather | solution.py:12
Sparse Core Ops, SparseCore 0:
  8.9 19.5 all-gather.3
  40.5 17.3 all-gather.5
  70.0 17.3 all-gather.7
where the time goes:
time: 107 us; the launch traced here: 106 us
  waiting for transfers between devices  55.9 us (52%)
  matrix products  35.7 us (33%)
  between operations  13.1 us (12%)
    all_gather x3, waiting for transfers between devices, local_stack(): x_full = lax.all_gather(x_cur, 'tp', axis=1, tiled=True)  55.2 us
    dot_general x3, matrix products, local_stack(): jnp.dot(x_full, w_loc[layer_idx], preferred_element_type=jnp.float32)  35.7 us
  transfers between devices with their start and end apart: 3, of which 3 were waited for; matrix products, arithmetic and copies ran while one was open for 1% of the time, Pallas kernels for 0%

commit v1 on v0

v1 whole, which is shorter than its diff:
```python
import functools

import jax
import jax.numpy as jnp
from jax import lax
from jax.experimental import pallas as pl
from jax.experimental.pallas import tpu as pltpu
from jax.sharding import PartitionSpec as P

MESH = pl.DeviceIdType.MESH
LAYERS, D, COLS, ROWS = 3, 6656, 1664, 128
HALF = ROWS // 2
TILE = 128
NT = COLS // TILE
OWN, MATE, FAR, FARMATE = range(4)
CHUNKS = ((0, 4), (4, 8), (8, 12), (12, 13))
NC = len(CHUNKS)


def tiles(role, chunk):
    return [(role, t) for t in range(*CHUNKS[chunk])]


SEGMENTS = [
    [(OWN, t) for t in range(NT)] + [(MATE, t) for t in range(NT)],
    tiles(FAR, 0),
    tiles(FAR, 1) + tiles(FARMATE, 0),
    tiles(FAR, 2) + tiles(FARMATE, 1),
    tiles(FARMATE, 2),
    tiles(FAR, 3) + tiles(FARMATE, 3),
]
SEQ = [t for s in SEGMENTS for t in s]
BLOCKS = [(SEQ[2 * i], SEQ[2 * i + 1]) for i in range(len(SEQ) // 2)]
NB = len(BLOCKS)
SEG_BLOCKS = []
_b = 0
for _s in SEGMENTS:
    SEG_BLOCKS.append(list(range(_b, _b + len(_s) // 2)))
    _b += len(_s) // 2
SLOTS = 65
NTILES = [(n, min(256, COLS - n)) for n in range(0, COLS, 256)]


def kernel(x_hbm, w_hbm, b_hbm, out_hbm, xb, wb, acc, bias, stage, w_sem, x_sem, b_sem, o_sem,
           far_send, far_recv, fwd_send, fwd_recv, mate_send, mate_recv):
    me = lax.axis_index("tp")
    mate = me + 1 - 2 * lax.rem(me, 2)
    far = lax.rem(me + 2, 4)
    farmate = lax.rem(mate + 2, 4)
    owners = (me, mate, far, farmate)

    def w_copies(layer, block, start):
        slot = lax.rem(layer * NB + block, SLOTS)
        (r0, t0), (r1, t1) = BLOCKS[block]
        if not start:
            pltpu.make_async_copy(w_hbm.at[0, pl.ds(0, 2 * TILE)], wb.at[slot], w_sem.at[slot]).wait()
        elif r0 == r1:
            row = pl.multiple_of(owners[r0] * COLS + t0 * TILE, TILE)
            pltpu.make_async_copy(w_hbm.at[layer, pl.ds(row, 2 * TILE)], wb.at[slot], w_sem.at[slot]).start()
        else:
            for i, (r, t) in enumerate(((r0, t0), (r1, t1))):
                row = pl.multiple_of(owners[r] * COLS + t * TILE, TILE)
                pltpu.make_async_copy(
                    w_hbm.at[layer, pl.ds(row, TILE)], wb.at[slot, pl.ds(i * TILE, TILE)], w_sem.at[slot]
                ).start()

    def far_copy(p, c):
        t0, t1 = CHUNKS[c]
        return pltpu.make_async_remote_copy(
            xb.at[p, pl.ds(OWN * NT + t0, t1 - t0)], xb.at[p, pl.ds(FAR * NT + t0, t1 - t0)],
            far_send.at[p, c], far_recv.at[p, c], device_id={"tp": far}, device_id_type=MESH)

    def fwd_copy(p, c):
        t0, t1 = CHUNKS[c]
        return pltpu.make_async_remote_copy(
            xb.at[p, pl.ds(FAR * NT + t0, t1 - t0)], xb.at[p, pl.ds(FARMATE * NT + t0, t1 - t0)],
            fwd_send.at[p, c], fwd_recv.at[p, c], device_id={"tp": mate}, device_id_type=MESH)

    def mate_copy(p):
        return pltpu.make_async_remote_copy(
            xb.at[p, pl.ds(OWN * NT, NT)], xb.at[p, pl.ds(MATE * NT, NT)],
            mate_send.at[p], mate_recv.at[p], device_id={"tp": mate}, device_id_type=MESH)

    for h in range(2):
        for t in range(NT):
            pltpu.make_async_copy(
                x_hbm.at[pl.ds(h * HALF, HALF), pl.ds(t * TILE, TILE)], xb.at[h, OWN * NT + t], x_sem.at[h]
            ).start()
    barrier = pltpu.get_barrier_semaphore()
    for other in (mate, far):
        pl.semaphore_signal(barrier, inc=1, device_id={"tp": other}, device_id_type=MESH)
    pltpu.make_async_copy(b_hbm, bias, b_sem).start()
    pl.semaphore_wait(barrier, 2)
    for h in range(2):
        pltpu.make_async_copy(xb.at[h, pl.ds(0, NT)], xb.at[h, pl.ds(0, NT)], x_sem.at[h]).wait()
        for c in range(NC):
            far_copy(h, c).start()
        mate_copy(h).start()
    for layer in range(LAYERS):
        for block in range(NB):
            if layer * NB + block < SLOTS:
                w_copies(layer, block, True)
    pltpu.make_async_copy(b_hbm, bias, b_sem).wait()

    def x_block(p, block):
        (r0, t0), (r1, t1) = BLOCKS[block]
        return jnp.concatenate([xb[p, r0 * NT + t0], xb[p, r1 * NT + t1]], axis=1)

    def dots(layer, p, blocks, n, width):
        total = None
        for block in blocks:
            slot = lax.rem(layer * NB + block, SLOTS)
            term = jnp.dot(x_block(p, block), wb[slot, :, pl.ds(n, width)], preferred_element_type=jnp.float32)
            total = term if total is None else total + term
        return total

    def phase(layer, h):
        p = 2 * layer + h

        def segment(s):
            if h == 0:
                for block in SEG_BLOCKS[s]:
                    w_copies(layer, block, False)
            for n, width in NTILES:
                part = dots(layer, p, SEG_BLOCKS[s], n, width)
                acc[:, pl.ds(n, width)] = part if s == 0 else acc[:, pl.ds(n, width)] + part

        mate_copy(p).wait_recv()
        segment(0)
        if h == 1:
            @pl.when(layer == 0)
            def _():
                for block in range(NB):
                    if 2 * NB + block >= SLOTS:
                        w_copies(2, block, True)
        far_copy(p, 0).wait_recv()
        fwd_copy(p, 0).start()
        segment(1)
        far_copy(p, 1).wait_recv()
        fwd_copy(p, 1).start()
        fwd_copy(p, 0).wait_recv()
        segment(2)
        far_copy(p, 2).wait_recv()
        fwd_copy(p, 2).start()
        fwd_copy(p, 1).wait_recv()
        segment(3)
        far_copy(p, 3).wait_recv()
        fwd_copy(p, 3).start()
        fwd_copy(p, 2).wait_recv()
        segment(4)
        for c in range(NC):
            far_copy(p, c).wait_send()
        mate_copy(p).wait_send()
        for c in range(NC - 1):
            fwd_copy(p, c).wait_send()
        if h == 0:
            for block in SEG_BLOCKS[5]:
                w_copies(layer, block, False)
        fwd_copy(p, 3).wait_recv()

        def result(n, width):
            projected = acc[:, pl.ds(n, width)] + dots(layer, p, SEG_BLOCKS[5], n, width)
            shift = bias[0:1, pl.ds(n, width)]
            for other in range(1, LAYERS):
                shift = jnp.where(layer == other, bias[other:other + 1, pl.ds(n, width)], shift)
            shifted = projected + shift
            parts = []
            for i in range(width // TILE):
                t = n // TILE + i
                first = xb[h, OWN * NT + t].astype(jnp.float32)
                now = xb[p, OWN * NT + t].astype(jnp.float32)
                parts.append((first * shifted[:, i * TILE:(i + 1) * TILE] + now).astype(jnp.bfloat16))
            return parts

        @pl.when(layer < LAYERS - 1)
        def _():
            sent = 0
            for n, width in NTILES:
                for i, part in enumerate(result(n, width)):
                    xb[p + 2, OWN * NT + n // TILE + i] = part
                done = (n + width) // TILE
                while sent < NC and CHUNKS[sent][1] <= done - 2:
                    far_copy(p + 2, sent).start()
                    sent += 1
            while sent < NC:
                far_copy(p + 2, sent).start()
                sent += 1
            mate_copy(p + 2).start()

        @pl.when(layer == LAYERS - 1)
        def _():
            for n, width in NTILES:
                for i, part in enumerate(result(n, width)):
                    stage[h, :, pl.ds(n + i * TILE, TILE)] = part
            pltpu.make_async_copy(stage.at[h], out_hbm.at[pl.ds(h * HALF, HALF)], o_sem.at[h]).start()

        fwd_copy(p, NC - 1).wait_send()

    def layer_step(layer, carry):
        phase(layer, 0)
        phase(layer, 1)
        return carry

    lax.fori_loop(0, LAYERS, layer_step, 0)
    for h in range(2):
        pltpu.make_async_copy(stage.at[h], out_hbm.at[pl.ds(h * HALF, HALF)], o_sem.at[h]).wait()


def solution(mesh):
    def local_stack(x_loc, w_loc, b_loc):
        any_space = pl.BlockSpec(memory_space=pl.ANY)
        sem = pltpu.SemaphoreType.DMA
        return pl.pallas_call(
            kernel,
            out_shape=jax.ShapeDtypeStruct((ROWS, COLS), jnp.bfloat16),
            in_specs=[any_space] * 3,
            out_specs=any_space,
            scratch_shapes=[
                pltpu.VMEM((2 * LAYERS, 4 * NT, HALF, TILE), jnp.bfloat16),
                pltpu.VMEM((SLOTS, 2 * TILE, COLS), jnp.bfloat16),
                pltpu.VMEM((HALF, COLS), jnp.float32),
                pltpu.VMEM((LAYERS, COLS), jnp.float32),
                pltpu.VMEM((2, HALF, COLS), jnp.bfloat16),
                sem((SLOTS,)), sem((2,)), sem, sem((2,)),
                sem((2 * LAYERS, NC)), sem((2 * LAYERS, NC)),
                sem((2 * LAYERS, NC)), sem((2 * LAYERS, NC)),
                sem((2 * LAYERS,)), sem((2 * LAYERS,)),
            ],
            compiler_params=pltpu.CompilerParams(
                collective_id=0, has_side_effects=True, vmem_limit_bytes=66_000_000
            ),
            name="cross_stack",
        )(x_loc, w_loc, b_loc)

    return jax.shard_map(
        local_stack,
        mesh=mesh,
        in_specs=(P("dp", "tp"), P(None, None, "tp"), P(None, "tp")),
        out_specs=P("dp", "tp"),
        check_vma=False,
    )
```

time: 107 us -> 47.4 us (0.44)
  the two profiles are of different devices: /device:TPU:1 before, /device:TPU:0 now
where the time goes in v1:
time: 47.4 us; the launch traced here: 47.2 us
  Pallas kernels  45.4 us (96%)
  local copies, waits for them, and re-layouts  1.8 us (4%)
    pallas_call x1, Pallas kernels, local_stack(): pl.pallas_call(kernel, out_shape=jax.ShapeDtypeStruct((ROWS, COLS), jnp.b...  45.4 us
    unnamed x1, local copies, waits for them, and re-layouts  1.8 us

profile of v1, /device:TPU:0, one launch (start us, length us, event | category | flops | bytes accessed | tf_op | source)
XLA Modules:
  0.0 47.2 jit_solution(14811335593944534447)
XLA Ops:
  0.0 45.4 %cross_stack.1 = bf16[128,1664]{1,0:T(8,128)(2,1)} custom-call(bf16[128,1664]{1,0:T(8,128)(2,1)} %x_hbm.1, bf16[3,6656,1664]{2,1,0:T(8,128)(2,1)} %w_hbm.1, f32[3,1664]{1,0:T(4,128)} %b_hbm.1), custom_call_target="tpu_custom_call" | custom-call | tf_op jit(solution)/shard_map/cross_stack/pallas_call | solution.py:213
  45.5 1.8 %copy.5 = bf16[128,1664]{1,0:T(8,128)(2,1)} copy(bf16[128,1664]{1,0:T(8,128)(2,1)} %cross_stack.1) | data formatting | bytes 851968

commit v2 on v1

--- a/solution.py
+++ b/solution.py
@@ -38,6 +38,7 @@
     SEG_BLOCKS.append(list(range(_b, _b + len(_s) // 2)))
     _b += len(_s) // 2
 SLOTS = 65
+AHEAD = ((3, 3, 3, 3, 2, 1), (3, 3, 2, 2, 1, 0))
 NTILES = [(n, min(256, COLS - n)) for n in range(0, COLS, 256)]
 
 
@@ -96,10 +97,8 @@
         for c in range(NC):
             far_copy(h, c).start()
         mate_copy(h).start()
-    for layer in range(LAYERS):
-        for block in range(NB):
-            if layer * NB + block < SLOTS:
-                w_copies(layer, block, True)
+    for block in range(NB):
+        w_copies(0, block, True)
     pltpu.make_async_copy(b_hbm, bias, b_sem).wait()
 
     def x_block(p, block):
@@ -124,15 +123,18 @@
             for n, width in NTILES:
                 part = dots(layer, p, SEG_BLOCKS[s], n, width)
                 acc[:, pl.ds(n, width)] = part if s == 0 else acc[:, pl.ds(n, width)] + part
+            ask(s)
+
+        def ask(s):
+            first = sum(AHEAD[0][:s]) if h == 0 else sum(AHEAD[0]) + sum(AHEAD[1][:s])
+
+            @pl.when(layer < LAYERS - 1)
+            def _():
+                for block in range(first, first + AHEAD[h][s]):
+                    w_copies(layer + 1, block, True)
 
         mate_copy(p).wait_recv()
         segment(0)
-        if h == 1:
-            @pl.when(layer == 0)
-            def _():
-                for block in range(NB):
-                    if 2 * NB + block >= SLOTS:
-                        w_copies(2, block, True)
         far_copy(p, 0).wait_recv()
         fwd_copy(p, 0).start()
         segment(1)
@@ -156,6 +158,7 @@
         if h == 0:
             for block in SEG_BLOCKS[5]:
                 w_copies(layer, block, False)
+        ask(5)
         fwd_copy(p, 3).wait_recv()
 
         def result(n, width):

time: 47.4 us -> 47.5 us (level)
  no operation moved by 1% of the time
where the time goes in v2:
time: 47.5 us; the launch traced here: 47.3 us
  Pallas kernels  45.5 us (96%)
  local copies, waits for them, and re-layouts  1.8 us (4%)
    pallas_call x1, Pallas kernels, local_stack(): pl.pallas_call(kernel, out_shape=jax.ShapeDtypeStruct((ROWS, COLS), jnp.b...  45.5 us
    unnamed x1, local copies, waits for them, and re-layouts  1.8 us

profile of v2, /device:TPU:0, one launch (start us, length us, event | category | flops | bytes accessed | tf_op | source)
XLA Modules:
  0.0 47.3 jit_solution(11585784029155432563)
XLA Ops:
  0.0 45.5 %cross_stack.1 = bf16[128,1664]{1,0:T(8,128)(2,1)} custom-call(bf16[128,1664]{1,0:T(8,128)(2,1)} %x_hbm.1, bf16[3,6656,1664]{2,1,0:T(8,128)(2,1)} %w_hbm.1, f32[3,1664]{1,0:T(4,128)} %b_hbm.1), custom_call_target="tpu_custom_call" | custom-call | tf_op jit(solution)/shard_map/cross_stack/pallas_call | solution.py:216
  45.5 1.8 %copy.5 = bf16[128,1664]{1,0:T(8,128)(2,1)} copy(bf16[128,1664]{1,0:T(8,128)(2,1)} %cross_stack.1) | data formatting | bytes 851968
